TPU v7x, 32 devices: a whole 2x2x4 slice. The times are simulated.
32 devices in a mesh: dp: 16 (over z, x, core), tensor: 2 (over y).
Axes of the slice: x: 2, y: 2, z: 4, core: 2. Of those that a mesh axis runs over, the one named last changes fastest.
Arguments:
- latent: bfloat16 [2, 32768, 1024], P(None, ('dp', 'tensor')), may hold values from -6 to 6
- embedding: bfloat16 [2, 32768, 1024], P(None, ('dp', 'tensor')), may hold values from -6 to 6
- prefix_len: int32 [2, 16], P(None, 'dp'), may hold values from 204 to 1024, as said below
- cotangent: bfloat16 [2, 32768, 1024], P(None, ('dp', 'tensor')), may hold values from -6 to 6
- adapter_w: bfloat16 [2048, 1024], P(('dp', 'tensor')), may hold values from -0.125 to 0.125
- pre_attn_gain: bfloat16 [1024], P(('dp', 'tensor')), may hold values from 0.25 to 1.75
- post_attn_gain: bfloat16 [1024], P(('dp', 'tensor')), may hold values from 0.25 to 1.75
- pre_mlp_gain: bfloat16 [1024], P(('dp', 'tensor')), may hold values from 0.25 to 1.75
- post_mlp_gain: bfloat16 [1024], P(('dp', 'tensor')), may hold values from 0.25 to 1.75
- query_w: bfloat16 [1024, 1024], P('dp', 'tensor'), may hold values from -0.375 to 0.375
- key_w: bfloat16 [1024, 1024], P('dp', 'tensor'), may hold values from -0.1875 to 0.1875
- value_w: bfloat16 [1024, 1024], P('dp', 'tensor'), may hold values from -0.1875 to 0.1875
- output_w: bfloat16 [1024, 1024], P('tensor', 'dp'), may hold values from -0.75 to 0.75
- gate_w: bfloat16 [1024, 2816], P('dp', 'tensor'), may hold values from -0.1875 to 0.1875
- up_w: bfloat16 [1024, 2816], P('dp', 'tensor'), may hold values from -0.1875 to 0.1875
- down_w: bfloat16 [2816, 1024], P('tensor', 'dp'), may hold values from -0.109375 to 0.109375
Outputs:
- layer_out: bfloat16 [2, 32768, 1024], P(None, ('dp', 'tensor'))
- latent_grad: bfloat16 [2, 32768, 1024], P(None, ('dp', 'tensor'))
- embedding_grad: bfloat16 [2, 32768, 1024], P(None, ('dp', 'tensor'))
- adapter_grad: float32 [2048, 1024], P(('dp', 'tensor'))
- pre_attn_grad: float32 [1024], P(('dp', 'tensor'))
- post_attn_grad: float32 [1024], P(('dp', 'tensor'))
- pre_mlp_grad: float32 [1024], P(('dp', 'tensor'))
- post_mlp_grad: float32 [1024], P(('dp', 'tensor'))
- query_grad: float32 [1024, 1024], P('dp', 'tensor')
- key_grad: float32 [1024, 1024], P('dp', 'tensor')
- value_grad: float32 [1024, 1024], P('dp', 'tensor')
- output_grad: float32 [1024, 1024], P('tensor', 'dp')
- gate_grad: float32 [1024, 2816], P('dp', 'tensor')
- up_grad: float32 [1024, 2816], P('dp', 'tensor')
- down_grad: float32 [2816, 1024], P('tensor', 'dp')
Inputs may be any that keep to these rules, and one draw needn't show every extreme that they name: `prefix_len`: some sequence has exactly 204 and some exactly 1024.
All inputs are finite; a program needn't handle non-finite values.
Results may differ from a plain program's by a relative error of at most 0.025.
Values may be sent and summed in bfloat16 or wider, within the bound.
A program may use at most 384 MiB of HBM per device.

v0:
```python
import jax
import jax.numpy as jnp
from jax import lax
from jax.sharding import PartitionSpec as P

HD = 128
LEN = 2048


EPS = 1e-06
THETA = 50000.0


def inner(left, right):
    return lax.dot_general(
        left, right, (((0,), (0,)), ((), ())), preferred_element_type=jnp.float32
    )


def outer_t(left, right):
    return lax.dot_general(
        left, right, (((1,), (1,)), ((), ())), preferred_element_type=jnp.float32
    )


def product(left, right):
    return jnp.dot(left, right, preferred_element_type=jnp.float32)


def normalize(values):
    factor = lax.rsqrt(jnp.mean(values * values, axis=-1, keepdims=True) + EPS)
    return (values * factor, factor)


def norm_back(scaled_grad, unit_rows, factor):
    return factor * (
        scaled_grad - unit_rows * jnp.mean(scaled_grad * unit_rows, axis=-1, keepdims=True)
    )


def rotary_tables(row_total):
    half_dim = HD // 2
    inv_freq = THETA ** (-(jnp.arange(half_dim, dtype=jnp.float32) * 2.0 / HD))
    positions = (jnp.arange(row_total, dtype=jnp.int32) % LEN).astype(jnp.float32)
    angles = positions[:, None] * inv_freq[None, :]
    return (jnp.cos(angles)[:, None, :], jnp.sin(angles)[:, None, :])


def rotate(values_in, cosine, sine_tab):
    half_dim = values_in.shape[-1] // 2
    leading = values_in[..., :half_dim]
    trailing = values_in[..., half_dim:]
    return jnp.concatenate(
        [leading * cosine - trailing * sine_tab, trailing * cosine + leading * sine_tab], axis=-1
    )


def rotate_back(values_in, cosine, sine_tab):
    half_dim = values_in.shape[-1] // 2
    leading = values_in[..., :half_dim]
    trailing = values_in[..., half_dim:]
    return jnp.concatenate(
        [leading * cosine + trailing * sine_tab, trailing * cosine - leading * sine_tab], axis=-1
    )


def masked_scores(query_blk, key_rows, block_idx, block_len, prefix_end):
    scaling = HD ** (-0.5)
    scores = (
        jnp.einsum("qhd,khd->hqk", query_blk, key_rows, preferred_element_type=jnp.float32)
        * scaling
    )
    key_pos = jnp.arange(LEN, dtype=jnp.int32)
    query_pos = block_idx * block_len + jnp.arange(block_len, dtype=jnp.int32)
    allowed = (key_pos[None, :] <= query_pos[:, None]) | (key_pos[None, :] < prefix_end)
    return jnp.where(allowed[None], scores, -1e30)


def attend(queries, keys_rot, value_rows, prefix_seq):
    row_total, head_count, head_dim = queries.shape
    seq_count = row_total // LEN
    block_len = min(512, LEN)
    blocks = LEN // block_len

    def one_seq(items):
        seq_idx, prefix_end = items

        def one_block(block_idx):
            query_blk = lax.dynamic_slice_in_dim(
                queries, seq_idx * LEN + block_idx * block_len, block_len, 0
            )
            scores = masked_scores(query_blk, keys_rot, block_idx, block_len, prefix_end)
            row_max = jnp.max(scores, axis=-1, keepdims=True)
            expo = jnp.exp(scores - row_max)
            row_sum = jnp.sum(expo, axis=-1, keepdims=True)
            weights = (expo / row_sum).astype(jnp.bfloat16)
            attn_blk = jnp.einsum(
                "hqk,khd->qhd", weights, value_rows, preferred_element_type=jnp.float32
            )
            return (attn_blk, (row_max + jnp.log(row_sum))[..., 0])

        attn_seq, lse_seq = lax.map(one_block, jnp.arange(blocks, dtype=jnp.int32))
        return (
            attn_seq.reshape(LEN, head_count * head_dim),
            jnp.transpose(lse_seq, (1, 0, 2)).reshape(head_count, LEN),
        )

    attn_all, lse_all = lax.map(one_seq, (jnp.arange(seq_count, dtype=jnp.int32), prefix_seq))
    return (attn_all.reshape(row_total, head_count * head_dim), lse_all)


def attend_back(queries, keys_rot, value_rows, lse_all, grad_attn, prefix_seq):
    row_total, head_count, head_dim = queries.shape
    seq_count = row_total // LEN
    block_len = min(512, LEN)
    blocks = LEN // block_len
    scaling = HD ** (-0.5)

    def one_seq(items):
        seq_idx, prefix_end, lse_seq = items

        def one_block(carry, block_idx):
            grad_key_acc, grad_val_acc = carry
            offset = seq_idx * LEN + block_idx * block_len
            query_blk = lax.dynamic_slice_in_dim(queries, offset, block_len, 0)
            grad_blk = lax.dynamic_slice_in_dim(grad_attn, offset, block_len, 0)
            scores = masked_scores(query_blk, keys_rot, block_idx, block_len, prefix_end)
            lse_blk = lax.dynamic_slice_in_dim(lse_seq, block_idx * block_len, block_len, 1)
            weights = jnp.exp(scores - lse_blk[..., None])
            grad_weights = jnp.einsum(
                "qhd,khd->hqk", grad_blk, value_rows, preferred_element_type=jnp.float32
            )
            row_dot = jnp.sum(weights * grad_weights, axis=-1, keepdims=True)
            grad_scores = (weights * (grad_weights - row_dot)).astype(jnp.bfloat16)
            grad_query = (
                jnp.einsum(
                    "hqk,khd->qhd", grad_scores, keys_rot, preferred_element_type=jnp.float32
                )
                * scaling
            )
            grad_key_acc = (
                grad_key_acc
                + jnp.einsum(
                    "hqk,qhd->khd", grad_scores, query_blk, preferred_element_type=jnp.float32
                )
                * scaling
            )
            grad_val_acc = grad_val_acc + jnp.einsum(
                "hqk,qhd->khd",
                weights.astype(jnp.bfloat16),
                grad_blk,
                preferred_element_type=jnp.float32,
            )
            return ((grad_key_acc, grad_val_acc), grad_query)

        zeros = jnp.zeros((LEN, head_count, head_dim), jnp.float32)
        sums, grad_queries = lax.scan(
            one_block, (zeros, zeros), jnp.arange(blocks, dtype=jnp.int32)
        )
        return (grad_queries.reshape(LEN, head_count, head_dim), sums[0], sums[1])

    grad_q, grad_k, grad_v = lax.map(
        one_seq, (jnp.arange(seq_count, dtype=jnp.int32), prefix_seq, lse_all)
    )
    shape = (row_total, head_count, head_dim)
    return (grad_q.reshape(shape), grad_k.reshape(shape), grad_v.reshape(shape))


def gather_weights(local_weights):
    (
        adapter_w,
        pre_attn_gain,
        post_attn_gain,
        pre_mlp_gain,
        post_mlp_gain,
        query_w,
        key_w,
        value_w,
        output_w,
        gate_w,
        up_w,
        down_w,
    ) = local_weights
    adapter_part = (
        lax.all_gather(adapter_w, ("dp", "tensor"), axis=0, tiled=True),
        lax.all_gather(pre_attn_gain, ("dp", "tensor"), axis=0, tiled=True),
        lax.all_gather(post_attn_gain, ("dp", "tensor"), axis=0, tiled=True),
        lax.all_gather(pre_mlp_gain, ("dp", "tensor"), axis=0, tiled=True),
        lax.all_gather(post_mlp_gain, ("dp", "tensor"), axis=0, tiled=True),
    )
    attn_part = (
        lax.all_gather(query_w, "dp", axis=0, tiled=True),
        lax.all_gather(key_w, "dp", axis=0, tiled=True),
        lax.all_gather(value_w, "dp", axis=0, tiled=True),
        lax.all_gather(output_w, "dp", axis=1, tiled=True),
    )
    mlp_part = (
        lax.all_gather(gate_w, "dp", axis=0, tiled=True),
        lax.all_gather(up_w, "dp", axis=0, tiled=True),
        lax.all_gather(down_w, "dp", axis=1, tiled=True),
    )
    return tuple(adapter_part) + tuple(attn_part) + tuple(mlp_part)


def micro_step(lat_rows, emb_rows, prefix_seq, cot_rows, gathered):
    (
        adapter_full,
        gain_one,
        gain_two,
        gain_three,
        gain_four,
        query_full,
        key_full,
        value_full,
        output_full,
        gate_full,
        up_full,
        down_full,
    ) = gathered
    gain_a = gain_one.astype(jnp.float32)
    gain_b = gain_two.astype(jnp.float32)
    gain_c = gain_three.astype(jnp.float32)
    gain_d = gain_four.astype(jnp.float32)
    joined = jnp.concatenate([lat_rows, emb_rows], axis=1)
    residual = product(joined, adapter_full)
    unit_one, factor_one = normalize(residual)
    attn_in = lax.all_gather((unit_one * gain_a).astype(jnp.bfloat16), "tensor", axis=0, tiled=True)
    row_total = attn_in.shape[0]
    head_count = query_full.shape[1] // HD
    cosine, sine_tab = rotary_tables(row_total)
    queries = rotate(
        product(attn_in, query_full).reshape(row_total, head_count, HD), cosine, sine_tab
    ).astype(jnp.bfloat16)
    keys_rot = rotate(
        product(attn_in, key_full).reshape(row_total, head_count, HD), cosine, sine_tab
    ).astype(jnp.bfloat16)
    value_rows = (
        product(attn_in, value_full).astype(jnp.bfloat16).reshape(row_total, head_count, HD)
    )
    attn_full, lse_all = attend(queries, keys_rot, value_rows, prefix_seq)
    attn_low = attn_full.astype(jnp.bfloat16)
    attn_proj = lax.psum_scatter(
        product(attn_low, output_full).astype(jnp.bfloat16),
        "tensor",
        scatter_dimension=0,
        tiled=True,
    ).astype(jnp.float32)
    unit_two, factor_two = normalize(attn_proj)
    middle = residual + unit_two * gain_b
    unit_three, factor_three = normalize(middle)
    mlp_in = lax.all_gather(
        (unit_three * gain_c).astype(jnp.bfloat16), "tensor", axis=0, tiled=True
    )
    gate_act = product(mlp_in, gate_full)
    up_act = product(mlp_in, up_full)
    hidden = (jax.nn.silu(gate_act) * up_act).astype(jnp.bfloat16)
    mlp_proj = lax.psum_scatter(
        product(hidden, down_full).astype(jnp.bfloat16), "tensor", scatter_dimension=0, tiled=True
    ).astype(jnp.float32)
    unit_four, factor_four = normalize(mlp_proj)
    result = middle + unit_four * gain_d
    grad_out = cot_rows.astype(jnp.float32)
    post_mlp_part = jnp.sum(grad_out * unit_four, axis=0)
    grad_mlp = norm_back(grad_out * gain_d, unit_four, factor_four).astype(jnp.bfloat16)
    grad_mlp_all = lax.all_gather(grad_mlp, "tensor", axis=0, tiled=True)
    down_part = inner(hidden, grad_mlp_all)
    grad_hidden = outer_t(grad_mlp_all, down_full)
    sigma = jax.nn.sigmoid(gate_act)
    grad_gate = (grad_hidden * up_act * sigma * (1.0 + gate_act * (1.0 - sigma))).astype(
        jnp.bfloat16
    )
    grad_up = (grad_hidden * gate_act * sigma).astype(jnp.bfloat16)
    gate_part = inner(mlp_in, grad_gate)
    up_part = inner(mlp_in, grad_up)
    grad_mlp_in = lax.psum_scatter(
        (outer_t(grad_gate, gate_full) + outer_t(grad_up, up_full)).astype(jnp.bfloat16),
        "tensor",
        scatter_dimension=0,
        tiled=True,
    ).astype(jnp.float32)
    pre_mlp_part = jnp.sum(grad_mlp_in * unit_three, axis=0)
    grad_middle = grad_out + norm_back(grad_mlp_in * gain_c, unit_three, factor_three)
    post_attn_part = jnp.sum(grad_middle * unit_two, axis=0)
    grad_proj = norm_back(grad_middle * gain_b, unit_two, factor_two).astype(jnp.bfloat16)
    grad_proj_all = lax.all_gather(grad_proj, "tensor", axis=0, tiled=True)
    output_part = inner(attn_low, grad_proj_all)
    grad_attn = (
        outer_t(grad_proj_all, output_full).astype(jnp.bfloat16).reshape(row_total, head_count, HD)
    )
    grad_q, grad_k, grad_v = attend_back(
        queries, keys_rot, value_rows, lse_all, grad_attn, prefix_seq
    )
    grad_q_raw = (
        rotate_back(grad_q, cosine, sine_tab)
        .astype(jnp.bfloat16)
        .reshape(row_total, head_count * HD)
    )
    grad_k_raw = (
        rotate_back(grad_k, cosine, sine_tab)
        .astype(jnp.bfloat16)
        .reshape(row_total, head_count * HD)
    )
    grad_values = grad_v.astype(jnp.bfloat16).reshape(row_total, head_count * HD)
    query_part = inner(attn_in, grad_q_raw)
    key_part = inner(attn_in, grad_k_raw)
    value_part = inner(attn_in, grad_values)
    grad_attn_in_part = (
        outer_t(grad_q_raw, query_full)
        + outer_t(grad_k_raw, key_full)
        + outer_t(grad_values, value_full)
    )
    grad_attn_in = lax.psum_scatter(
        grad_attn_in_part.astype(jnp.bfloat16), "tensor", scatter_dimension=0, tiled=True
    ).astype(jnp.float32)
    pre_attn_part = jnp.sum(grad_attn_in * unit_one, axis=0)
    grad_residual = (grad_middle + norm_back(grad_attn_in * gain_a, unit_one, factor_one)).astype(
        jnp.bfloat16
    )
    adapter_part = inner(joined, grad_residual)
    grad_joined = outer_t(grad_residual, adapter_full)
    width = lat_rows.shape[1]
    latent_grad = grad_joined[:, :width].astype(jnp.bfloat16)
    embedding_grad = grad_joined[:, width:].astype(jnp.bfloat16)
    partials = (
        adapter_part,
        pre_attn_part,
        post_attn_part,
        pre_mlp_part,
        post_mlp_part,
        query_part,
        key_part,
        value_part,
        output_part,
        gate_part,
        up_part,
        down_part,
    )
    return (result.astype(jnp.bfloat16), latent_grad, embedding_grad, partials)


def local(
    latent,
    embedding,
    prefix_len,
    cotangent,
    adapter_w,
    pre_attn_gain,
    post_attn_gain,
    pre_mlp_gain,
    post_mlp_gain,
    query_w,
    key_w,
    value_w,
    output_w,
    gate_w,
    up_w,
    down_w,
):
    local_weights = (
        adapter_w,
        pre_attn_gain,
        post_attn_gain,
        pre_mlp_gain,
        post_mlp_gain,
        query_w,
        key_w,
        value_w,
        output_w,
        gate_w,
        up_w,
        down_w,
    )
    batches = latent.shape[0]
    layer_rows = []
    latent_rows = []
    embed_rows = []
    totals = None
    for micro in range(batches):
        current = gather_weights(local_weights)
        result, lat_grad, emb_grad, partials = micro_step(
            latent[micro], embedding[micro], prefix_len[micro], cotangent[micro], current
        )
        layer_rows.append(result)
        latent_rows.append(lat_grad)
        embed_rows.append(emb_grad)
        if totals is None:
            totals = partials
        else:
            totals = jax.tree.map(lambda left, right: left + right, totals, partials)
    adapter_grad, pre_attn_grad, post_attn_grad, pre_mlp_grad, post_mlp_grad = (
        lax.psum_scatter(totals[0], ("dp", "tensor"), scatter_dimension=0, tiled=True),
        lax.psum_scatter(totals[1], ("dp", "tensor"), scatter_dimension=0, tiled=True),
        lax.psum_scatter(totals[2], ("dp", "tensor"), scatter_dimension=0, tiled=True),
        lax.psum_scatter(totals[3], ("dp", "tensor"), scatter_dimension=0, tiled=True),
        lax.psum_scatter(totals[4], ("dp", "tensor"), scatter_dimension=0, tiled=True),
    )
    query_grad, key_grad, value_grad, output_grad = (
        lax.psum_scatter(
            totals[5].astype(jnp.bfloat16), "dp", scatter_dimension=0, tiled=True
        ).astype(jnp.float32),
        lax.psum_scatter(
            totals[6].astype(jnp.bfloat16), "dp", scatter_dimension=0, tiled=True
        ).astype(jnp.float32),
        lax.psum_scatter(
            totals[7].astype(jnp.bfloat16), "dp", scatter_dimension=0, tiled=True
        ).astype(jnp.float32),
        lax.psum_scatter(
            totals[8].astype(jnp.bfloat16), "dp", scatter_dimension=1, tiled=True
        ).astype(jnp.float32),
    )
    gate_grad, up_grad, down_grad = (
        lax.psum_scatter(
            totals[9].astype(jnp.bfloat16), "dp", scatter_dimension=0, tiled=True
        ).astype(jnp.float32),
        lax.psum_scatter(
            totals[10].astype(jnp.bfloat16), "dp", scatter_dimension=0, tiled=True
        ).astype(jnp.float32),
        lax.psum_scatter(
            totals[11].astype(jnp.bfloat16), "dp", scatter_dimension=1, tiled=True
        ).astype(jnp.float32),
    )
    return (
        jnp.stack(layer_rows),
        jnp.stack(latent_rows),
        jnp.stack(embed_rows),
        adapter_grad,
        pre_attn_grad,
        post_attn_grad,
        pre_mlp_grad,
        post_mlp_grad,
        query_grad,
        key_grad,
        value_grad,
        output_grad,
        gate_grad,
        up_grad,
        down_grad,
    )


def solution(mesh):
    placed = (
        P(None, ("dp", "tensor"), None),
        P(None, ("dp", "tensor"), None),
        P(None, "dp"),
        P(None, ("dp", "tensor"), None),
        P(("dp", "tensor"), None),
        P(("dp", "tensor")),
        P(("dp", "tensor")),
        P(("dp", "tensor")),
        P(("dp", "tensor")),
        P("dp", "tensor"),
        P("dp", "tensor"),
        P("dp", "tensor"),
        P("tensor", "dp"),
        P("dp", "tensor"),
        P("dp", "tensor"),
        P("tensor", "dp"),
    )
    return jax.shard_map(
        local,
        mesh=mesh,
        in_specs=placed,
        out_specs=(
            P(None, ("dp", "tensor"), None),
            P(None, ("dp", "tensor"), None),
            P(None, ("dp", "tensor"), None),
            P(("dp", "tensor"), None),
            P(("dp", "tensor")),
            P(("dp", "tensor")),
            P(("dp", "tensor")),
            P(("dp", "tensor")),
            P("dp", "tensor"),
            P("dp", "tensor"),
            P("dp", "tensor"),
            P("tensor", "dp"),
            P("dp", "tensor"),
            P("dp", "tensor"),
            P("tensor", "dp"),
        ),
        check_vma=False,
    )
```

profile of v0, /device:TPU:0, one launch (start us, length us, event | category | flops | bytes accessed | tf_op | source)
XLA Modules:
  0.0 2855.3 jit_solution(5503634215058759566)
XLA Ops:
  12.1 42.1 %all-reduce.9 = (bf16[1024]{0:T(1024)(128)(2,1)S(1)}, bf16[1024]{0:T(1024)(128)(2,1)}, bf16[1024]{0:T(1024)(128)(2,1)}, bf16[1024]{0:T(1024)(128)(2,1)}) all-reduce(bf16[1024]{0:T(1024)(128)(2,1)S(1)} %dynamic-update-slice, bf16[1024]{0:T(1024)(128)(2,1)S(1)} %dynamic-update-slice.1, ...), channel_id=1, replica_groups=mesh['dp'=16,'tensor'=2] {'dp','tensor'}, use_global_device_ids=true, to_apply=%add | all-reduce | flops 4096 | bytes 16384
  114.2 57.9 %all-gather.19.cloned.1.call-done = bf16[2048,1024]{0,1:T(8,128)(2,1)} async-done(((bf16[1024,1024]{0,1:T(8,128)(2,1)}), bf16[2048,1024]{0,1:T(8,128)(2,1)}) %all-gather.19.cloned.1.call-update) | async-done | bytes 4194320 | tf_op jit(solution)/shard_map/all_gather | solution.py:227
  179.0 33.0 %all-gather.23.cloned.1.call-done = bf16[1024,512]{1,0:T(8,128)(2,1)} async-done(((bf16[64,512]{1,0:T(8,128)(2,1)}), bf16[1024,512]{1,0:T(8,128)(2,1)}) %all-gather.23.cloned.1.call-update) | async-done | bytes 1048592 | tf_op jit(solution)/shard_map/all_gather | solution.py:193
  262.7 71.5 %while.106 = (s32[]{:T(128)}, bf16[4,512,4,128]{3,1,2,0:T(8,128)(2,1)}, f32[4,4,512]{2,1,0:T(4,128)S(1)}, s32[4]{0:T(128)S(1)}, s32[]{:T(128)}, /*index=5*/bf16[...) while((s32[]{:T(128)}, ...), condition=%wide.region_4.5_spmd, body=%wide.region_1.4_spmd.sunk | while | flops 2199912960 | bytes 68756184 | solution.py:102
  346.8 52.6 %reduce-scatter.17.cloned.1.call-done = bf16[1024,1024]{0,1:T(8,128)(2,1)} async-done(((bf16[2048,1024]{0,1:T(8,128)(2,1)}), bf16[1024,1024]{0,1:T(8,128)(2,1)}) %reduce-scatter.17.cloned.1.call-update) | async-done | bytes 2097168 | tf_op jit(solution)/shard_map/reduce_scatter | solution.py:242
  410.4 35.3 %all-gather.31.cloned.1.call-done = bf16[1024,1408]{1,0:T(8,128)(2,1)} async-done(((bf16[64,1408]{1,0:T(8,128)(2,1)}), bf16[1024,1408]{1,0:T(8,128)(2,1)}) %all-gather.31.cloned.1.call-update) | async-done | bytes 2883600 | tf_op jit(solution)/shard_map/all_gather | solution.py:198
  445.7 57.5 %all-gather.29.cloned.1.call-done = bf16[2048,1024]{0,1:T(8,128)(2,1)} async-done(((bf16[1024,1024]{0,1:T(8,128)(2,1)}), bf16[2048,1024]{0,1:T(8,128)(2,1)}) %all-gather.29.cloned.1.call-update) | async-done | bytes 4194320 | tf_op jit(solution)/shard_map/all_gather | solution.py:251
  515.6 33.7 %all-gather.33.cloned.1.call-done = bf16[1024,1408]{1,0:T(8,128)(2,1)} async-done(((bf16[64,1408]{1,0:T(8,128)(2,1)}), bf16[1024,1408]{1,0:T(8,128)(2,1)}) %all-gather.33.cloned.1.call-update) | async-done | bytes 2883600 | tf_op jit(solution)/shard_map/all_gather | solution.py:199
  565.2 29.0 %all-gather.35.cloned.1.call-done = bf16[1408,1024]{0,1:T(8,128)(2,1)} async-done(((bf16[1408,64]{0,1:T(8,128)(2,1)}), bf16[1408,1024]{0,1:T(8,128)(2,1)}) %all-gather.35.cloned.1.call-update) | async-done | bytes 2883600 | tf_op jit(solution)/shard_map/all_gather | solution.py:200
  613.9 44.9 %reduce-scatter.19.cloned.1.call-done = bf16[1024,1024]{0,1:T(8,128)(2,1)} async-done(((bf16[2048,1024]{0,1:T(8,128)(2,1)}), bf16[1024,1024]{0,1:T(8,128)(2,1)}) %reduce-scatter.19.cloned.1.call-update) | async-done | bytes 2097168 | tf_op jit(solution)/shard_map/reduce_scatter | solution.py:257
  667.0 56.8 %all-gather.41.cloned.1.call-done = bf16[2048,1024]{0,1:T(8,128)(2,1)} async-done(((bf16[1024,1024]{0,1:T(8,128)(2,1)}), bf16[2048,1024]{0,1:T(8,128)(2,1)}) %all-gather.41.cloned.1.call-update) | async-done | bytes 4194320 | tf_op jit(solution)/shard_map/all_gather | solution.py:265
  762.8 53.9 %reduce-scatter.25.cloned.1.call-done = bf16[1024,1024]{0,1:T(8,128)(2,1)} async-done(((bf16[2048,1024]{0,1:T(8,128)(2,1)}), bf16[1024,1024]{0,1:T(8,128)(2,1)}) %reduce-scatter.25.cloned.1.call-update) | async-done | bytes 2097168 | tf_op jit(solution)/shard_map/reduce_scatter | solution.py:275
  833.1 41.7 %all-gather.37.cloned.1.call-done = bf16[2048,1024]{0,1:T(8,128)(2,1)} async-done(((bf16[1024,1024]{0,1:T(8,128)(2,1)}), bf16[2048,1024]{0,1:T(8,128)(2,1)}) %all-gather.37.cloned.1.call-update) | async-done | bytes 4194320 | tf_op jit(solution)/shard_map/all_gather | solution.py:227
  893.6 39.3 %all-gather.43.cloned.1.call-done = bf16[2048,1024]{0,1:T(8,128)(2,1)} async-done(((bf16[1024,1024]{0,1:T(8,128)(2,1)}), bf16[2048,1024]{0,1:T(8,128)(2,1)}) %all-gather.43.cloned.1.call-update) | async-done | bytes 4194320 | tf_op jit(solution)/shard_map/all_gather | solution.py:285
  938.9 365.7 %while.108 = (s32[]{:T(128)}, f32[2048,4,128]{0,2,1:T(8,128)}, f32[2048,4,128]{0,2,1:T(8,128)}, f32[4,512,4,128]{1,0,3,2:T(4,128)}, s32[4]{0:T(128)S(1)}, /*inde...) while((s32[]{:T(128)}, f32[2048,4,128]{0,2,1:T(8,128)}, ...), condition=%wide.region_26.27_spmd.clone, body=%wide.region_24.26_spmd.clone.sunk | while | flops 5439226368 | bytes 202441008 | solution.py:157
  987.1 21.1 dynamic_update_slice.84
  1332.5 71.3 %while.107 = (s32[]{:T(128)}, bf16[4,512,4,128]{3,1,2,0:T(8,128)(2,1)}, f32[4,4,512]{2,1,0:T(4,128)S(1)}, s32[4]{0:T(128)S(1)}, s32[]{:T(128)}, /*index=5*/bf16[...) while((s32[]{:T(128)}, ...), condition=%wide.region_14.15_spmd, body=%wide.region_11.14_spmd.sunk | while | flops 2199912960 | bytes 68756184 | solution.py:102
  1413.7 54.5 %reduce-scatter.21.cloned.1.call-done = bf16[1024,1024]{0,1:T(8,128)(2,1)} async-done(((bf16[2048,1024]{0,1:T(8,128)(2,1)}), bf16[1024,1024]{0,1:T(8,128)(2,1)}) %reduce-scatter.21.cloned.1.call-update) | async-done | bytes 2097168 | tf_op jit(solution)/shard_map/reduce_scatter | solution.py:242
  1477.9 56.8 %all-gather.39.cloned.1.call-done = bf16[2048,1024]{0,1:T(8,128)(2,1)} async-done(((bf16[1024,1024]{0,1:T(8,128)(2,1)}), bf16[2048,1024]{0,1:T(8,128)(2,1)}) %all-gather.39.cloned.1.call-update) | async-done | bytes 4194320 | tf_op jit(solution)/shard_map/all_gather | solution.py:251
  1575.2 51.6 %reduce-scatter.23.cloned.1.call-done = bf16[1024,1024]{0,1:T(8,128)(2,1)} async-done(((bf16[2048,1024]{0,1:T(8,128)(2,1)}), bf16[1024,1024]{0,1:T(8,128)(2,1)}) %reduce-scatter.23.cloned.1.call-update) | async-done | bytes 2097168 | tf_op jit(solution)/shard_map/reduce_scatter | solution.py:257
  1635.0 56.8 %all-gather.45.cloned.1.call-done = bf16[2048,1024]{0,1:T(8,128)(2,1)} async-done(((bf16[1024,1024]{0,1:T(8,128)(2,1)}), bf16[2048,1024]{0,1:T(8,128)(2,1)}) %all-gather.45.cloned.1.call-update) | async-done | bytes 4194320 | tf_op jit(solution)/shard_map/all_gather | solution.py:265
  1730.3 54.5 %reduce-scatter.29.cloned.1.call-done = bf16[1024,1024]{0,1:T(8,128)(2,1)} async-done(((bf16[2048,1024]{0,1:T(8,128)(2,1)}), bf16[1024,1024]{0,1:T(8,128)(2,1)}) %reduce-scatter.29.cloned.1.call-update) | async-done | bytes 2097168 | tf_op jit(solution)/shard_map/reduce_scatter | solution.py:275
  1815.4 42.7 %all-gather.47.cloned.1.call-done = bf16[2048,1024]{0,1:T(8,128)(2,1)} async-done(((bf16[1024,1024]{0,1:T(8,128)(2,1)}), bf16[2048,1024]{0,1:T(8,128)(2,1)}) %all-gather.47.cloned.1.call-update) | async-done | bytes 4194320 | tf_op jit(solution)/shard_map/all_gather | solution.py:285
  1864.0 266.0 %while.109 = (s32[]{:T(128)}, f32[2048,4,128]{0,2,1:T(8,128)}, f32[2048,4,128]{0,2,1:T(8,128)}, f32[4,512,4,128]{3,1,0,2:T(8,128)}, s32[4]{0:T(128)S(1)}, /*inde...) while((s32[]{:T(128)}, f32[2048,4,128]{0,2,1:T(8,128)}, ...), condition=%wide.region_35.36_spmd.clone, body=%wide.region_33.35_spmd.clone.sunk | while | flops 5439226368 | bytes 198247216 | solution.py:157
  2292.0 61.0 %reduce-scatter.45.cloned.1.call-done = bf16[64,1408]{1,0:T(8,128)(2,1)} async-done(((bf16[1024,1408]{1,0:T(8,128)(2,1)}), bf16[64,1408]{1,0:T(8,128)(2,1)}) %reduce-scatter.45.cloned.1.call-update) | async-done | bytes 180240 | tf_op jit(solution)/shard_map/reduce_scatter | solution.py:415
  2354.7 66.9 %reduce-scatter.43.cloned.1.call-done = bf16[64,1408]{1,0:T(8,128)(2,1)} async-done(((bf16[1024,1408]{1,0:T(8,128)(2,1)}), bf16[64,1408]{1,0:T(8,128)(2,1)}) %reduce-scatter.43.cloned.1.call-update) | async-done | bytes 180240 | tf_op jit(solution)/shard_map/reduce_scatter | solution.py:412
  2433.6 48.2 %reduce-scatter.41.cloned.1.call-done = bf16[512,64]{0,1:T(8,128)(2,1)} async-done(((bf16[512,1024]{0,1:T(8,128)(2,1)}), bf16[512,64]{0,1:T(8,128)(2,1)}) %reduce-scatter.41.cloned.1.call-update) | async-done | bytes 65552 | tf_op jit(solution)/shard_map/reduce_scatter | solution.py:407
  2483.3 58.8 %reduce-scatter.39.cloned.1.call-done = bf16[64,512]{1,0:T(8,128)(2,1)} async-done(((bf16[1024,512]{1,0:T(8,128)(2,1)}), bf16[64,512]{1,0:T(8,128)(2,1)}) %reduce-scatter.39.cloned.1.call-update) | async-done | bytes 65552 | tf_op jit(solution)/shard_map/reduce_scatter | solution.py:404
  2543.6 58.7 %reduce-scatter.37.cloned.1.call-done = bf16[64,512]{1,0:T(8,128)(2,1)} async-done(((bf16[1024,512]{1,0:T(8,128)(2,1)}), bf16[64,512]{1,0:T(8,128)(2,1)}) %reduce-scatter.37.cloned.1.call-update) | async-done | bytes 65552 | tf_op jit(solution)/shard_map/reduce_scatter | solution.py:401
  2603.8 58.8 %reduce-scatter.35.cloned.1.call-done = bf16[64,512]{1,0:T(8,128)(2,1)} async-done(((bf16[1024,512]{1,0:T(8,128)(2,1)}), bf16[64,512]{1,0:T(8,128)(2,1)}) %reduce-scatter.35.cloned.1.call-update) | async-done | bytes 65552 | tf_op jit(solution)/shard_map/reduce_scatter | solution.py:398
  2664.1 41.5 %all-reduce.8 = (f32[1024]{0:T(1024)S(1)}, f32[1024]{0:T(1024)S(1)}, f32[1024]{0:T(1024)S(1)}, f32[1024]{0:T(1024)S(1)}) all-reduce(f32[1024]{0:T(1024)S(1)} %add.545, f32[1024]{0:T(1024)S(1)} %add.546, f32[1024]{0:T(1024)S(1)} %add.547, f32[1024]{0:T(1024)S(1)} %add.548), channel_id=11, replica_groups=mesh['dp'=16,'tensor'=2] {'dp','tensor'}, use_global_device_ids=true, to_apply=%region_41.42.clone | all-reduce | flops 4096 | bytes 32768
  2727.8 120.7 %reduce-scatter.33.cloned.1.call-done = f32[64,1024]{1,0:T(8,128)} async-done(((f32[2048,1024]{1,0:T(8,128)}), f32[64,1024]{1,0:T(8,128)}) %reduce-scatter.33.cloned.1.call-update) | async-done | bytes 262160 | tf_op jit(solution)/shard_map/reduce_scatter | solution.py:391
  (678 shorter events, 1396.8 us)
Async XLA Ops:
  7.2 68.2 %all-gather.17.cloned.1.call-start = ((), (), s32[]{:S(2)}) async-start(), calls=%async_computation.16 | async-start | bytes 4325376 | tf_op jit(solution)/shard_map/all_gather | solution.py:185
  7.9 106.3 %all-gather.21.cloned.1.call-start = ((), (), s32[]{:S(2)}) async-start(), calls=%async_computation.18 | async-start | bytes 1114112 | tf_op jit(solution)/shard_map/all_gather | solution.py:192
  8.7 163.4 %all-gather.19.cloned.1.call-start = ((), (), s32[]{:S(2)}) async-start(), calls=%async_computation.17 | async-start | bytes 6291456 | tf_op jit(solution)/shard_map/all_gather | solution.py:227
  90.6 121.3 %all-gather.23.cloned.1.call-start = ((), (), s32[]{:S(2)}) async-start(), calls=%async_computation.19 | async-start | bytes 1114112 | tf_op jit(solution)/shard_map/all_gather | solution.py:193
  91.2 159.6 %all-gather.25.cloned.1.call-start = ((), (), s32[]{:S(2)}) async-start(), calls=%async_computation.20 | async-start | bytes 1114112 | tf_op jit(solution)/shard_map/all_gather | solution.py:194
  91.8 247.8 %all-gather.27.cloned.1.call-start = ((), (), s32[]{:S(2)}) async-start(), calls=%async_computation.21 | async-start | bytes 1114112 | tf_op jit(solution)/shard_map/all_gather | solution.py:195
  92.4 307.0 %reduce-scatter.17.cloned.1.call-start = ((), (), s32[]{:S(2)}) async-start(), calls=%async_computation.22 | async-start | bytes 6291456 | tf_op jit(solution)/shard_map/reduce_scatter | solution.py:242
  345.9 99.8 %all-gather.31.cloned.1.call-start = ((), (), s32[]{:S(2)}) async-start(), calls=%async_computation.24 | async-start | bytes 3063808 | tf_op jit(solution)/shard_map/all_gather | solution.py:198
  346.7 156.5 %all-gather.29.cloned.1.call-start = ((), (), s32[]{:S(2)}) async-start(), calls=%async_computation.23 | async-start | bytes 6291456 | tf_op jit(solution)/shard_map/all_gather | solution.py:251
  409.0 140.3 %all-gather.33.cloned.1.call-start = ((), (), s32[]{:S(2)}) async-start(), calls=%async_computation.25 | async-start | bytes 3063808 | tf_op jit(solution)/shard_map/all_gather | solution.py:199
  409.6 184.6 %all-gather.35.cloned.1.call-start = ((), (), s32[]{:S(2)}) async-start(), calls=%async_computation.26 | async-start | bytes 3063808 | tf_op jit(solution)/shard_map/all_gather | solution.py:200
  410.3 248.4 %reduce-scatter.19.cloned.1.call-start = ((), (), s32[]{:S(2)}) async-start(), calls=%async_computation.27 | async-start | bytes 6291456 | tf_op jit(solution)/shard_map/reduce_scatter | solution.py:257
  605.6 118.2 %all-gather.41.cloned.1.call-start = ((), (), s32[]{:S(2)}) async-start(), calls=%async_computation.32 | async-start | bytes 6291456 | tf_op jit(solution)/shard_map/all_gather | solution.py:265
  666.9 149.7 %reduce-scatter.25.cloned.1.call-start = ((), (), s32[]{:S(2)}) async-start(), calls=%async_computation.33 | async-start | bytes 6291456 | tf_op jit(solution)/shard_map/reduce_scatter | solution.py:275
  762.1 112.7 %all-gather.37.cloned.1.call-start = ((), (), s32[]{:S(2)}) async-start(), calls=%async_computation.28 | async-start | bytes 6291456 | tf_op jit(solution)/shard_map/all_gather | solution.py:227
  762.7 170.2 %all-gather.43.cloned.1.call-start = ((), (), s32[]{:S(2)}) async-start(), calls=%async_computation.34 | async-start | bytes 6291456 | tf_op jit(solution)/shard_map/all_gather | solution.py:285
  833.0 635.1 %reduce-scatter.21.cloned.1.call-start = ((), (), s32[]{:S(2)}) async-start(), calls=%async_computation.29 | async-start | bytes 6291456 | tf_op jit(solution)/shard_map/reduce_scatter | solution.py:242
  1413.6 121.1 %all-gather.39.cloned.1.call-start = ((), (), s32[]{:S(2)}) async-start(), calls=%async_computation.30 | async-start | bytes 6291456 | tf_op jit(solution)/shard_map/all_gather | solution.py:251
  1477.8 149.0 %reduce-scatter.23.cloned.1.call-start = ((), (), s32[]{:S(2)}) async-start(), calls=%async_computation.31 | async-start | bytes 6291456 | tf_op jit(solution)/shard_map/reduce_scatter | solution.py:257
  1572.3 119.6 %all-gather.45.cloned.1.call-start = ((), (), s32[]{:S(2)}) async-start(), calls=%async_computation.36 | async-start | bytes 6291456 | tf_op jit(solution)/shard_map/all_gather | solution.py:265
  1635.0 149.8 %reduce-scatter.29.cloned.1.call-start = ((), (), s32[]{:S(2)}) async-start(), calls=%async_computation.37 | async-start | bytes 6291456 | tf_op jit(solution)/shard_map/reduce_scatter | solution.py:275
  1730.2 127.9 %all-gather.47.cloned.1.call-start = ((), (), s32[]{:S(2)}) async-start(), calls=%async_computation.38 | async-start | bytes 6291456 | tf_op jit(solution)/shard_map/all_gather | solution.py:285
  1801.3 456.3 %reduce-scatter.27.cloned.1.call-start = ((), (), s32[]{:S(2)}) async-start(), calls=%async_computation.35 | async-start | bytes 6291456 | tf_op jit(solution)/shard_map/reduce_scatter | solution.py:312
  1815.4 452.4 %reduce-scatter.31.cloned.1.call-start = ((), (), s32[]{:S(2)}) async-start(), calls=%async_computation.39 | async-start | bytes 6291456 | tf_op jit(solution)/shard_map/reduce_scatter | solution.py:312
  2161.6 128.7 %reduce-scatter.47.cloned.1.call-start = ((), (), s32[]{:S(2)}) async-start(), calls=%async_computation.47 | async-start | bytes 3063808 | tf_op jit(solution)/shard_map/reduce_scatter | solution.py:418
  2183.1 169.8 %reduce-scatter.45.cloned.1.call-start = ((), (), s32[]{:S(2)}) async-start(), calls=%async_computation.46 | async-start | bytes 3063808 | tf_op jit(solution)/shard_map/reduce_scatter | solution.py:415
  2204.6 217.0 %reduce-scatter.43.cloned.1.call-start = ((), (), s32[]{:S(2)}) async-start(), calls=%async_computation.45 | async-start | bytes 3063808 | tf_op jit(solution)/shard_map/reduce_scatter | solution.py:412
  2226.3 255.5 %reduce-scatter.41.cloned.1.call-start = ((), (), s32[]{:S(2)}) async-start(), calls=%async_computation.44 | async-start | bytes 1114112 | tf_op jit(solution)/shard_map/reduce_scatter | solution.py:407
  2234.6 307.5 %reduce-scatter.39.cloned.1.call-start = ((), (), s32[]{:S(2)}) async-start(), calls=%async_computation.43 | async-start | bytes 1114112 | tf_op jit(solution)/shard_map/reduce_scatter | solution.py:404
  2243.4 358.9 %reduce-scatter.37.cloned.1.call-start = ((), (), s32[]{:S(2)}) async-start(), calls=%async_computation.42 | async-start | bytes 1114112 | tf_op jit(solution)/shard_map/reduce_scatter | solution.py:401
  2251.6 410.9 %reduce-scatter.35.cloned.1.call-start = ((), (), s32[]{:S(2)}) async-start(), calls=%async_computation.41 | async-start | bytes 1114112 | tf_op jit(solution)/shard_map/reduce_scatter | solution.py:398
  2267.5 581.0 %reduce-scatter.33.cloned.1.call-start = ((), (), s32[]{:S(2)}) async-start(), calls=%async_computation.40 | async-start | bytes 8650752 | tf_op jit(solution)/shard_map/reduce_scatter | solution.py:391
  (141 other events, 3171.9 us)
Sparse Core Ops, SparseCore 0:
  10.9 64.4 all-gather.16
  77.5 36.6 all-gather.20
  116.4 55.6 all-gather.18
  174.1 37.8 all-gather.22
  214.0 36.8 all-gather.24
  252.8 36.8 all-gather.26
  346.0 53.3 reduce-scatter.16
  401.7 43.9 all-gather.30
  447.8 55.3 all-gather.28
  505.3 43.9 all-gather.32
  551.6 42.5 all-gather.34
  605.7 52.9 reduce-scatter.18
  667.0 56.7 all-gather.40
  762.3 54.3 reduce-scatter.24
  818.1 56.7 all-gather.36
  876.2 56.7 all-gather.42
  1413.7 54.3 reduce-scatter.20
  1477.9 56.7 all-gather.38
  1572.4 54.3 reduce-scatter.22
  1635.1 56.6 all-gather.44
  1730.3 54.3 reduce-scatter.28
  1801.4 56.7 all-gather.46
  1860.4 54.3 reduce-scatter.26
  2161.7 54.2 reduce-scatter.30
  2219.8 65.1 reduce-scatter.46
  2288.7 64.2 reduce-scatter.44
  2357.2 64.2 reduce-scatter.42
  2425.1 56.6 reduce-scatter.40
  2485.5 56.5 reduce-scatter.38
  2545.6 56.6 reduce-scatter.36
  2605.9 56.5 reduce-scatter.34
  2665.4 183.0 reduce-scatter.32
where the time goes:
time: 2870 us; the launch traced here: 2860 us
  waiting for transfers between devices  1390 us (48%)
  matrix products  831 us (29%)
  other arithmetic  294 us (10%)
  local copies, waits for them, and re-layouts  231 us (8%)
  blocking collectives  83.6 us (3%)
    dot_general x16, matrix products, product(): return jnp.dot(left, right, preferred_element_type=jnp.float32)  132 us
    reduce_scatter x1, waiting for transfers between devices, local(): lax.psum_scatter(totals[0], ('dp', 'tensor'), scatter_dimension=0, tiled=...  121 us
    dot_general x16, matrix products, outer_t(): lax.dot_general(left, right, (((1,), (1,)), ((), ())), preferred_element_...  118 us
    all_gather x2, waiting for transfers between devices, micro_step(): lax.all_gather((unit_three * gain_c).astype(jnp.bfloat16), 'tensor', axis...  114 us
    all_gather x2, waiting for transfers between devices, micro_step(): grad_mlp_all = lax.all_gather(grad_mlp, 'tensor', axis=0, tiled=True)  114 us
    dot_general x16, matrix products, inner(): lax.dot_general(left, right, (((0,), (0,)), ((), ())), preferred_element_...  112 us
    dot_general x8, matrix products, one_block(): jnp.einsum('hqk,qhd->khd', weights.astype(jnp.bfloat16), grad_blk, prefer...  111 us
    dot_general x16, matrix products, masked_scores(): jnp.einsum('qhd,khd->hqk', query_blk, key_rows, preferred_element_type=jn...  111 us
  transfers between devices with their start and end apart: 32, of which 28 were waited for; matrix products, arithmetic and copies ran while one was open for 24% of the time, Pallas kernels for 0%

commit v1 on v0

--- a/solution.py
+++ b/solution.py
@@ -1,6 +1,10 @@
+import functools
+
 import jax
 import jax.numpy as jnp
 from jax import lax
+from jax.experimental import pallas as pl
+from jax.experimental.pallas import tpu as pltpu
 from jax.sharding import PartitionSpec as P
 
 HD = 128
@@ -438,6 +442,446 @@
     )
 
 
+BLK = 512
+LOG2E = 1.4426950408889634
+NEG = -1e30
+
+
+def turn(values, cosine, signed_sine):
+    return values * cosine + pltpu.roll(values, HD // 2, 1) * signed_sine
+
+
+def visible(row_start, key_start, row_axis, prefix_end):
+    rows = row_start + lax.broadcasted_iota(jnp.int32, (BLK, BLK), row_axis)
+    keys = key_start + lax.broadcasted_iota(jnp.int32, (BLK, BLK), 1 - row_axis)
+    return (keys <= rows) | (keys < prefix_end)
+
+
+def attend_kernel(
+    info, q_own, q_oth, k_own, k_oth, v_own, v_oth, cos_ref, sin_ref,
+    attn_ref, lse_ref, q_ref, k_ref, v_ref, wide, acc, peak,
+):
+    side, prefix_end = info[0], info[1]
+    half = q_own.shape[0]
+    length = 2 * half
+    blocks = length // BLK
+    factor = LOG2E * HD**-0.5
+
+    def stored(block):
+        return pl.multiple_of(lax.rem(block * BLK + side * half, length), BLK)
+
+    for slot, (q_in, k_in, v_in) in enumerate(((q_own, k_own, v_own), (q_oth, k_oth, v_oth))):
+        place = side if slot == 0 else 1 - side
+        rows = pl.ds(pl.multiple_of(place * half, half), half)
+        cosine, signed_sine = cos_ref[rows, :], sin_ref[rows, :]
+        here = pl.ds(slot * half, half)
+        q_ref[here, :] = turn(q_in[...], cosine, signed_sine).astype(jnp.bfloat16)
+        k_ref[here, :] = turn(k_in[...], cosine, signed_sine).astype(jnp.bfloat16)
+        v_ref[here, :] = v_in[...]
+        wide[here, :HD] = v_in[...]
+        wide[here, HD:] = jnp.ones((half, HD), jnp.bfloat16)
+
+    for row_block in range(blocks):
+        mine = pl.ds(stored(row_block), BLK)
+        acc[...] = jnp.zeros_like(acc)
+        peak[...] = jnp.full_like(peak, NEG)
+
+        def step(key_block, masked):
+            keys = pl.ds(stored(key_block), BLK)
+            scores = outer_t(q_ref[mine, :], k_ref[keys, :]) * factor
+            if masked:
+                seen = visible(row_block * BLK, key_block * BLK, 0, prefix_end)
+                scores = jnp.where(seen, scores, NEG)
+            old = peak[:, :1]
+            top = jnp.maximum(old, jnp.max(scores, axis=1, keepdims=True))
+            weights = jnp.exp2(scores - top).astype(jnp.bfloat16)
+            acc[...] = acc[...] * jnp.exp2(old - top) + product(weights, wide[keys, :])
+            peak[...] = jnp.broadcast_to(top, peak.shape)
+
+        clear = jnp.maximum(row_block, prefix_end // BLK)
+        last = jnp.maximum(row_block + 1, (prefix_end + BLK - 1) // BLK)
+
+        def plain(key_block, carry):
+            step(key_block, False)
+            return carry
+
+        def edged(key_block, carry):
+            step(key_block, True)
+            return carry
+
+        lax.fori_loop(0, clear, plain, 0)
+        lax.fori_loop(clear, last, edged, 0)
+        total = acc[:, HD:]
+        attn_ref[mine, :] = (acc[:, :HD] / total).astype(jnp.bfloat16)
+        lse_ref[0, :, mine] = jnp.transpose(peak[...] + jnp.log2(total))[:8]
+
+
+def attend_back_kernel(
+    info, q_ref, k_ref, v_ref, attn_ref, lse_ref, go_own, go_oth, cos_ref, sin_ref,
+    grad_ref, go_ref, delta, dq, dk, dv,
+):
+    side, prefix_end = info[0], info[1]
+    head = pl.program_id(0)
+    heads = grad_ref.shape[1] // (3 * HD)
+    half = go_own.shape[0]
+    length = 2 * half
+    blocks = length // BLK
+    factor = LOG2E * HD**-0.5
+    scaling = HD**-0.5
+
+    def stored(block):
+        return pl.multiple_of(lax.rem(block * BLK + side * half, length), BLK)
+
+    go_ref[:half, :] = go_own[...]
+    go_ref[half:, :] = go_oth[...]
+    for block in range(blocks):
+        here = pl.ds(block * BLK, BLK)
+        both = go_ref[here, :].astype(jnp.float32) * attn_ref[here, :].astype(jnp.float32)
+        sums = jnp.sum(jnp.transpose(both), axis=0, keepdims=True)
+        delta[:, here] = jnp.broadcast_to(sums, (8, BLK))
+    dq[...] = jnp.zeros_like(dq)
+
+    for key_block in range(blocks):
+        keys = pl.ds(stored(key_block), BLK)
+        dk[...] = jnp.zeros_like(dk)
+        dv[...] = jnp.zeros_like(dv)
+
+        def step(row_block, masked):
+            rows = pl.ds(stored(row_block), BLK)
+            queries, grads = q_ref[rows, :], go_ref[rows, :]
+            scores = outer_t(k_ref[keys, :], queries) * factor - lse_ref[0, :1, rows]
+            if masked:
+                seen = visible(row_block * BLK, key_block * BLK, 1, prefix_end)
+                scores = jnp.where(seen, scores, NEG)
+            weights = jnp.exp2(scores)
+            slope = outer_t(v_ref[keys, :], grads) - delta[:1, rows]
+            low = (weights * slope).astype(jnp.bfloat16)
+            dv[...] += product(weights.astype(jnp.bfloat16), grads)
+            dk[...] += product(low, queries)
+            dq[rows, :] += inner(low, k_ref[keys, :])
+
+        whole = (key_block + 1) * BLK <= prefix_end
+        reached = key_block * BLK < prefix_end
+        first = jnp.where(reached, 0, key_block)
+        clear = jnp.where(whole, 0, key_block + 1)
+
+        def plain(row_block, carry):
+            step(row_block, False)
+            return carry
+
+        def edged(row_block, carry):
+            step(row_block, True)
+            return carry
+
+        lax.fori_loop(first, clear, edged, 0)
+        lax.fori_loop(clear, blocks, plain, 0)
+        place = pl.ds(pl.multiple_of(key_block * BLK, BLK), BLK)
+        back = turn(dk[...] * scaling, cos_ref[place, :], -sin_ref[place, :])
+        columns = pl.ds(pl.multiple_of((heads + head) * HD, HD), HD)
+        grad_ref[keys, columns] = back.astype(jnp.bfloat16)
+        columns = pl.ds(pl.multiple_of((2 * heads + head) * HD, HD), HD)
+        grad_ref[keys, columns] = dv[...].astype(jnp.bfloat16)
+
+    for block in range(blocks):
+        rows = pl.ds(stored(block), BLK)
+        place = pl.ds(block * BLK, BLK)
+        back = turn(dq[rows, :] * scaling, cos_ref[place, :], -sin_ref[place, :])
+        columns = pl.ds(pl.multiple_of(head * HD, HD), HD)
+        grad_ref[rows, columns] = back.astype(jnp.bfloat16)
+
+
+def head_columns(rows, shift=0):
+    return pl.BlockSpec((rows, HD), lambda head, info: (0, head + shift))
+
+
+def fixed(rows, columns):
+    return pl.BlockSpec((rows, columns), lambda head, info: (0, 0))
+
+
+def attend_half(info, qk_own, qk_oth, v_own, v_oth, tables):
+    half = qk_own.shape[0]
+    heads = v_own.shape[1] // HD
+    length = 2 * half
+    low = jax.ShapeDtypeStruct((length, heads * HD), jnp.bfloat16)
+    pairs = heads * length * length * 0.6
+    return pl.pallas_call(
+        attend_kernel,
+        grid_spec=pltpu.PrefetchScalarGridSpec(
+            num_scalar_prefetch=1,
+            grid=(heads,),
+            in_specs=[
+                head_columns(half), head_columns(half),
+                head_columns(half, heads), head_columns(half, heads),
+                head_columns(half), head_columns(half),
+                fixed(length, HD), fixed(length, HD),
+            ],
+            out_specs=[
+                head_columns(length),
+                pl.BlockSpec((1, 8, length), lambda head, info: (head, 0, 0)),
+                head_columns(length), head_columns(length), head_columns(length),
+            ],
+            scratch_shapes=[
+                pltpu.VMEM((length, 2 * HD), jnp.bfloat16),
+                pltpu.VMEM((BLK, 2 * HD), jnp.float32),
+                pltpu.VMEM((BLK, HD), jnp.float32),
+            ],
+        ),
+        out_shape=(low, jax.ShapeDtypeStruct((heads, 8, length), jnp.float32), low, low, low),
+        cost_estimate=pl.CostEstimate(
+            flops=int(pairs * 8 * HD), bytes_accessed=int(40 * length * heads * HD), transcendentals=int(pairs)
+        ),
+        name="attend",
+    )(info, qk_own, qk_oth, qk_own, qk_oth, v_own, v_oth, *tables)
+
+
+def attend_back_half(info, saved, go_own, go_oth, tables):
+    attn, lse, queries, keys_rot, value_rows = saved
+    half = go_own.shape[0]
+    heads = go_own.shape[1] // HD
+    length = 2 * half
+    pairs = heads * length * length * 0.6
+    return pl.pallas_call(
+        attend_back_kernel,
+        grid_spec=pltpu.PrefetchScalarGridSpec(
+            num_scalar_prefetch=1,
+            grid=(heads,),
+            in_specs=[
+                head_columns(length), head_columns(length), head_columns(length), head_columns(length),
+                pl.BlockSpec((1, 8, length), lambda head, info: (head, 0, 0)),
+                head_columns(half), head_columns(half),
+                fixed(length, HD), fixed(length, HD),
+            ],
+            out_specs=fixed(length, 3 * heads * HD),
+            scratch_shapes=[
+                pltpu.VMEM((length, HD), jnp.bfloat16),
+                pltpu.VMEM((8, length), jnp.float32),
+                pltpu.VMEM((length, HD), jnp.float32),
+                pltpu.VMEM((BLK, HD), jnp.float32),
+                pltpu.VMEM((BLK, HD), jnp.float32),
+            ],
+        ),
+        out_shape=jax.ShapeDtypeStruct((length, 3 * heads * HD), jnp.bfloat16),
+        cost_estimate=pl.CostEstimate(
+            flops=int(pairs * 20 * HD), bytes_accessed=int(16 * length * heads * HD), transcendentals=int(pairs)
+        ),
+        name="attend_back",
+    )(info, queries, keys_rot, value_rows, attn, lse, go_own, go_oth, *tables)
+
+
+def swap(values):
+    return lax.ppermute(values, "tensor", [(0, 1), (1, 0)])
+
+
+def low(values):
+    return values.astype(jnp.bfloat16)
+
+
+def total_over(parts, side):
+    mine = lax.psum_scatter(parts, "dp", scatter_dimension=0, tiled=True)
+    width = mine.shape[1] // 2
+    lower, upper = mine[:, :width], mine[:, width:]
+    sent = jnp.where(side == 0, upper, lower)
+    kept = jnp.where(side == 0, lower, upper)
+    return kept.astype(jnp.float32) + swap(sent).astype(jnp.float32)
+
+
+def fast_local(
+    latent, embedding, prefix_len, cotangent, adapter_w, pre_attn_gain, post_attn_gain,
+    pre_mlp_gain, post_mlp_gain, query_w, key_w, value_w, output_w, gate_w, up_w, down_w,
+):
+    side = lax.axis_index("tensor")
+    dp_size, both = lax.axis_size("dp"), ("dp", "tensor")
+    half, width = latent.shape[1:]
+    shard = adapter_w.shape[0]
+    gain_len = pre_attn_gain.shape[0]
+    quarter = query_w.shape[1]
+    inner_len = gate_w.shape[1]
+
+    gains_row = jnp.concatenate([pre_attn_gain, post_attn_gain, pre_mlp_gain, post_mlp_gain])
+    gains_block = jnp.pad(gains_row[None, :], ((0, shard - 1), (0, 0)))
+    first = lax.all_gather(jnp.concatenate([adapter_w, gains_block], axis=1), both, axis=0, tiled=True)
+    attn_w = lax.all_gather(
+        jnp.concatenate([query_w, key_w, value_w, output_w.T], axis=1), ("tensor", "dp"), axis=0, tiled=True
+    ).reshape(2, width, -1)
+    mlp_w = lax.all_gather(
+        jnp.concatenate([gate_w, up_w, down_w.T], axis=1), ("tensor", "dp"), axis=0, tiled=True
+    ).reshape(2, width, -1)
+    adapter_top, adapter_bottom = first[:width, :width], first[width:, :width]
+    gains = first[::shard, width:].reshape(-1, 4, gain_len).transpose(1, 0, 2).reshape(4, width)
+    gain_a, gain_b, gain_c, gain_d = (gains[i].astype(jnp.float32) for i in range(4))
+
+    info = jnp.stack([side.astype(jnp.int32), jnp.where(side == 0, prefix_len[0, 0], prefix_len[1, 0])])
+    half_dim = HD // 2
+    inv_freq = THETA ** (-(jnp.arange(half_dim, dtype=jnp.float32) * 2.0 / HD))
+    angles = jnp.arange(2 * half, dtype=jnp.float32)[:, None] * inv_freq[None, :]
+    cosine, sine = jnp.cos(angles), jnp.sin(angles)
+    tables = (jnp.concatenate([cosine, cosine], axis=1), jnp.concatenate([-sine, sine], axis=1))
+
+    def pick(values, index):
+        return lax.dynamic_index_in_dim(values, index, 0, keepdims=False)
+
+    order = (side, 1 - side)
+    lat = [pick(latent, i) for i in order]
+    emb = [pick(embedding, i) for i in order]
+    cot = [pick(cotangent, i) for i in order]
+
+    def enter(slot):
+        residual = product(lat[slot], adapter_top) + product(emb[slot], adapter_bottom)
+        unit, factor = normalize(residual)
+        return residual, unit, factor, low(unit * gain_a)
+
+    res_o, unit_one_o, factor_one_o, attn_in_sent = enter(1)
+    attn_in_oth = swap(attn_in_sent)
+    res_m, unit_one_m, factor_one_m, attn_in_own = enter(0)
+
+    def project(rows, part):
+        weights = attn_w[part]
+        return (
+            product(rows, weights[:, : 2 * quarter]),
+            low(product(rows, weights[:, 2 * quarter : 3 * quarter])),
+        )
+
+    own = [project(attn_in_own, part) for part in range(2)]
+    oth = [project(attn_in_oth, part) for part in range(2)]
+    saved = [
+        attend_half(info, own[p][0], oth[p][0], own[p][1], oth[p][1], tables) for p in range(2)
+    ]
+    out_w = [attn_w[p][:, 3 * quarter :] for p in range(2)]
+
+    def project_out(rows):
+        return outer_t(saved[0][0][rows], out_w[0]) + outer_t(saved[1][0][rows], out_w[1])
+
+    proj_o = swap(low(project_out(slice(half, None)))).astype(jnp.float32)
+    proj_m = low(project_out(slice(0, half))).astype(jnp.float32)
+
+    gate_w_all = [mlp_w[p][:, :inner_len] for p in range(2)]
+    up_w_all = [mlp_w[p][:, inner_len : 2 * inner_len] for p in range(2)]
+    down_w_all = [mlp_w[p][:, 2 * inner_len :] for p in range(2)]
+
+    def feed(residual, attn_proj, cot_rows):
+        unit_two, factor_two = normalize(attn_proj)
+        middle = residual + unit_two * gain_b
+        unit_three, factor_three = normalize(middle)
+        mlp_in = low(unit_three * gain_c)
+        acts = []
+        mlp_proj = None
+        for p in range(2):
+            gate_act = product(mlp_in, gate_w_all[p])
+            up_act = product(mlp_in, up_w_all[p])
+            hidden = low(jax.nn.silu(gate_act) * up_act)
+            acts.append((gate_act, up_act, hidden))
+            part = outer_t(hidden, down_w_all[p])
+            mlp_proj = part if mlp_proj is None else mlp_proj + part
+        unit_four, factor_four = normalize(mlp_proj)
+        result = low(middle + unit_four * gain_d)
+        grad_out = cot_rows.astype(jnp.float32)
+        post_mlp_part = jnp.sum(grad_out * unit_four, axis=0)
+        grad_mlp = low(norm_back(grad_out * gain_d, unit_four, factor_four))
+        grads = []
+        grad_mlp_in = None
+        for p in range(2):
+            gate_act, up_act, hidden = acts[p]
+            grad_hidden = product(grad_mlp, down_w_all[p])
+            sigma = jax.nn.sigmoid(gate_act)
+            grad_gate = low(grad_hidden * up_act * sigma * (1.0 + gate_act * (1.0 - sigma)))
+            grad_up = low(grad_hidden * gate_act * sigma)
+            grads.append((grad_gate, grad_up, hidden))
+            part = outer_t(grad_gate, gate_w_all[p]) + outer_t(grad_up, up_w_all[p])
+            grad_mlp_in = part if grad_mlp_in is None else grad_mlp_in + part
+        pre_mlp_part = jnp.sum(grad_mlp_in * unit_three, axis=0)
+        grad_middle = grad_out + norm_back(grad_mlp_in * gain_c, unit_three, factor_three)
+        post_attn_part = jnp.sum(grad_middle * unit_two, axis=0)
+        grad_proj = low(norm_back(grad_middle * gain_b, unit_two, factor_two))
+        return result, grad_middle, grad_proj, mlp_in, grad_mlp, grads, (
+            post_attn_part, pre_mlp_part, post_mlp_part,
+        )
+
+    result_m, grad_middle_m, grad_proj_own, mlp_in_m, grad_mlp_m, grads_m, sums_m = feed(
+        res_m, proj_m, cot[0]
+    )
+    result_o, grad_middle_o, grad_proj_sent, mlp_in_o, grad_mlp_o, grads_o, sums_o = feed(
+        res_o, proj_o, cot[1]
+    )
+    grad_proj_oth = swap(grad_proj_sent)
+    mlp_cols = []
+    for p in range(2):
+        for i in range(2):
+            mlp_cols.append(low(inner(mlp_in_m, grads_m[p][i]) + inner(mlp_in_o, grads_o[p][i])))
+        mlp_cols.append(low(inner(grad_mlp_m, grads_m[p][2]) + inner(grad_mlp_o, grads_o[p][2])))
+    mlp_total = total_over(jnp.concatenate(mlp_cols, axis=1), side)
+
+    grad_qkv = []
+    for p in range(2):
+        go_own = low(product(grad_proj_own, out_w[p]))
+        go_oth = low(product(grad_proj_oth, out_w[p]))
+        grad_qkv.append(attend_back_half(info, saved[p], go_own, go_oth, tables))
+
+    in_w = [attn_w[p][:, : 3 * quarter] for p in range(2)]
+
+    def grad_in(rows):
+        return outer_t(grad_qkv[0][rows], in_w[0]) + outer_t(grad_qkv[1][rows], in_w[1])
+
+    grad_in_o = swap(low(grad_in(slice(half, None)))).astype(jnp.float32)
+    grad_in_m = low(grad_in(slice(0, half))).astype(jnp.float32)
+    attn_cols = []
+    for p in range(2):
+        mine, others = slice(0, half), slice(half, None)
+        attn_cols.append(
+            low(inner(attn_in_own, grad_qkv[p][mine]) + inner(attn_in_oth, grad_qkv[p][others]))
+        )
+        attn_cols.append(
+            low(inner(grad_proj_own, saved[p][0][mine]) + inner(grad_proj_oth, saved[p][0][others]))
+        )
+    attn_total = total_over(jnp.concatenate(attn_cols, axis=1), side)
+
+    def leave(grad_attn_in, unit_one, factor_one, grad_middle):
+        part = jnp.sum(grad_attn_in * unit_one, axis=0)
+        grad_residual = low(grad_middle + norm_back(grad_attn_in * gain_a, unit_one, factor_one))
+        return (
+            grad_residual, part,
+            low(outer_t(grad_residual, adapter_top)), low(outer_t(grad_residual, adapter_bottom)),
+        )
+
+    grad_res_m, pre_m, lat_grad_m, emb_grad_m = leave(grad_in_m, unit_one_m, factor_one_m, grad_middle_m)
+    grad_res_o, pre_o, lat_grad_o, emb_grad_o = leave(grad_in_o, unit_one_o, factor_one_o, grad_middle_o)
+    top = low(inner(lat[0], grad_res_m) + inner(lat[1], grad_res_o))
+    bottom = low(inner(emb[0], grad_res_m) + inner(emb[1], grad_res_o))
+    gain_sums = jnp.stack([pre_m + pre_o] + [sums_m[i] + sums_o[i] for i in range(3)])
+    gain_sums = low(gain_sums).reshape(4, -1, gain_len).transpose(1, 0, 2).reshape(-1, 1, 4 * gain_len)
+    gain_sums = jnp.pad(gain_sums, ((0, 0), (0, shard - 1), (0, 0))).reshape(-1, 4 * gain_len)
+    last = jnp.concatenate([jnp.concatenate([top, bottom], axis=0), gain_sums], axis=1)
+    last = lax.psum_scatter(last, "dp", scatter_dimension=0, tiled=True)
+    sent = jnp.where(side == 0, last[shard:], last[:shard])
+    kept = jnp.where(side == 0, last[:shard], last[shard:])
+    last = kept.astype(jnp.float32) + swap(sent).astype(jnp.float32)
+    gain_grads = [last[0, width + i * gain_len : width + (i + 1) * gain_len] for i in range(4)]
+
+    def join(mine, others):
+        return jnp.stack([jnp.where(side == 0, mine, others), jnp.where(side == 0, others, mine)])
+
+    return (
+        join(result_m, result_o),
+        join(lat_grad_m, lat_grad_o),
+        join(emb_grad_m, emb_grad_o),
+        last[:, :width],
+        *gain_grads,
+        attn_total[:, :quarter],
+        attn_total[:, quarter : 2 * quarter],
+        attn_total[:, 2 * quarter : 3 * quarter],
+        attn_total[:, 3 * quarter :].T,
+        mlp_total[:, :inner_len],
+        mlp_total[:, inner_len : 2 * inner_len],
+        mlp_total[:, 2 * inner_len :].T,
+    )
+
+
+def choose(*arguments):
+    latent, prefix_len, query_w = arguments[0], arguments[2], arguments[9]
+    paired = lax.axis_size("tensor") == 2 and latent.shape[0] == 2
+    whole = 2 * latent.shape[1] == LEN and prefix_len.shape[1] == 1 and query_w.shape[1] % HD == 0
+    return fast_local(*arguments) if paired and whole else local(*arguments)
+
+
 def solution(mesh):
     placed = (
         P(None, ("dp", "tensor"), None),
@@ -458,7 +902,7 @@
         P("tensor", "dp"),
     )
     return jax.shard_map(
-        local,
+        choose,
         mesh=mesh,
         in_specs=placed,
         out_specs=(

time: 2870 us -> 1270 us (0.44)
  waiting for transfers between devices: 1390 us -> 459 us
  matrix products: 831 us -> 421 us
  Pallas kernels: 0 us -> 232 us
  other arithmetic: 294 us -> 80.4 us
  local copies, waits for them, and re-layouts: 231 us -> 42.9 us
  blocking collectives: 83.6 us -> 0 us
    reduce_scatter x16 -> x3, waiting for transfers between devices: 785 us -> 212 us  [the longest x2 212 us: total_over(): mine = lax.psum_scatter(parts, 'dp', scatter_dimension=0, tiled=True)]
    dot_general x56 -> x0, matrix products: 469 us -> none  [the longest x8 111 us: one_block(): jnp.einsum('hqk,qhd->khd', weights.astype(jnp.bfloat16), grad_blk, prefer...]
    all_gather x16 -> x3, waiting for transfers between devices: 595 us -> 133 us  [the longest x1 68.2 us: fast_local(): lax.all_gather(jnp.concatenate([query_w, key_w, value_w, output_w.T], axi...]
    pallas_call x0 -> x4, Pallas kernels: none -> 232 us  [the longest x2 129 us: attend_half(): pl.pallas_call(attend_kernel, grid_spec=pltpu.PrefetchScalarGridSpec(num_...]
    convert_element_type x30 -> x7, other arithmetic: 142 us -> 18.6 us  [the longest x6 18.4 us: low(): return values.astype(jnp.bfloat16)]
    ppermute x0 -> x7, waiting for transfers between devices: none -> 114 us  [swap(): return lax.ppermute(values, 'tensor', [(0, 1), (1, 0)])]
    dynamic_update_slice x8 -> x0, local copies, waits for them, and re-layouts: 98.7 us -> none  [one_seq(): attn_seq, lse_seq = lax.map(one_block, jnp.arange(blocks, dtype=jnp.int32))]
    unnamed x2 -> x0, blocking collectives: 83.6 us -> none
  transfers between devices with their start and end apart: 32 -> 13, of which waited for: 28 -> 8; matrix products, arithmetic and copies ran while one was open for 24% -> 22% of each run, Pallas kernels for 0% -> 10%
where the time goes in v1:
time: 1270 us; the launch traced here: 1260 us
  waiting for transfers between devices  459 us (36%)
  matrix products  421 us (33%)
  Pallas kernels  232 us (18%)
  other arithmetic  80.4 us (6%)
  local copies, waits for them, and re-layouts  42.9 us (3%)
  between operations  17.3 us (1%)
    reduce_scatter x2, waiting for transfers between devices, total_over(): mine = lax.psum_scatter(parts, 'dp', scatter_dimension=0, tiled=True)  212 us
    dot_general x28, matrix products, product(): return jnp.dot(left, right, preferred_element_type=jnp.float32)  172 us
    dot_general x24, matrix products, outer_t(): lax.dot_general(left, right, (((1,), (1,)), ((), ())), preferred_element_...  144 us
    pallas_call x2, Pallas kernels, attend_half(): pl.pallas_call(attend_kernel, grid_spec=pltpu.PrefetchScalarGridSpec(num_...  129 us
    ppermute x7, waiting for transfers between devices, swap(): return lax.ppermute(values, 'tensor', [(0, 1), (1, 0)])  114 us
    dot_general x24, matrix products, inner(): lax.dot_general(left, right, (((0,), (0,)), ((), ())), preferred_element_...  105 us
    pallas_call x2, Pallas kernels, attend_back_half(): pl.pallas_call(attend_back_kernel, grid_spec=pltpu.PrefetchScalarGridSpec...  103 us
    all_gather x1, waiting for transfers between devices, fast_local(): lax.all_gather(jnp.concatenate([query_w, key_w, value_w, output_w.T], axi...  68.2 us
  transfers between devices with their start and end apart: 13, of which 8 were waited for; matrix products, arithmetic and copies ran while one was open for 22% of the time, Pallas kernels for 10%

profile of v1, /device:TPU:0, one launch (start us, length us, event | category | flops | bytes accessed | tf_op | source)
XLA Modules:
  0.0 1260.9 jit_solution(15738535893543345711)
XLA Ops:
  13.5 64.4 %all-gather.4.cloned.1.call-done = bf16[2048,1152]{1,0:T(8,128)(2,1)} async-done(((bf16[64,1152]{1,0:T(8,128)(2,1)}), bf16[2048,1152]{1,0:T(8,128)(2,1)}) %all-gather.4.cloned.1.call-update) | async-done | bytes 4718608 | tf_op jit(solution)/shard_map/all_gather | solution.py:702
  105.4 68.2 %all-gather.6.cloned.1.call-done = bf16[2048,2048]{1,0:T(8,128)(2,1)} async-done(((bf16[64,2048]{1,0:T(8,128)(2,1)}), bf16[2048,2048]{1,0:T(8,128)(2,1)}) %all-gather.6.cloned.1.call-update) | async-done | bytes 8388624 | tf_op jit(solution)/shard_map/all_gather | solution.py:703
  192.0 16.1 %fusion.142.q_oth.k_oth = f32[1024,1024]{1,0:T(8,128)} fusion(bf16[1024,1024]{0,1:T(8,128)(2,1)} %collective-permute-done, bf16[2048,2048]{1,0:T(8,128)(2,1)S(1)} %copy-done.40), kind=kOutput, calls=%fused_computation.219 | convolution fusion | flops 2147483648 | bytes 8388608 | tf_op jit(solution)/shard_map/dot_general | solution.py:31
  208.1 64.4 %attend.2 = (bf16[2048,512]{1,0:T(8,128)(2,1)}, f32[4,8,2048]{2,1,0:T(8,128)}, bf16[2048,512]{1,0:T(8,128)(2,1)}, bf16[2048,512]{1,0:T(8,128)(2,1)}, bf16[2048,512]{1,0:T(8,128)(2,1)}) custom-call(s32[2]{0:T(128)} %pad_add_fusion.info, f32[1024,1024]{1,0:T(8,128)} %fusion.144.q_own.k_own, f32[1024,1024]{1,0:T(8,128)} %fusion.142.q_oth.k_oth, ...), custom_call_target="tpu_custom_call" | custom-call | flops 10307921920 | bytes 41943040 | tf_op jit(solution)/shard_map/attend/pallas_call | solution.py:607
  290.2 64.8 %attend.3 = (bf16[2048,512]{1,0:T(8,128)(2,1)}, f32[4,8,2048]{2,1,0:T(8,128)}, bf16[2048,512]{1,0:T(8,128)(2,1)}, bf16[2048,512]{1,0:T(8,128)(2,1)}, bf16[2048,512]{1,0:T(8,128)(2,1)}) custom-call(s32[2]{0:T(128)} %pad_add_fusion.info, f32[1024,1024]{1,0:T(8,128)} %fusion.140.q_own.k_own, f32[1024,1024]{1,0:T(8,128)} %fusion.138.q_oth.k_oth, ...), custom_call_target="tpu_custom_call" | custom-call | flops 10307921920 | bytes 41943040 | tf_op jit(solution)/shard_map/attend/pallas_call | solution.py:607
  377.6 31.0 %collective-permute-done.1 = bf16[1024,1024]{0,1:T(8,128)(2,1)} collective-permute-done((bf16[1024,1024]{0,1:T(8,128)(2,1)}, bf16[1024,1024]{0,1:T(8,128)(2,1)}, u32[]{:S(2)}, u32[]{:S(2)}) %collective-permute-start.1) | collective-permute-done | bytes 2097184 | tf_op jit(solution)/shard_map/ppermute | solution.py:672
  425.7 9.3 fusion.112
  441.5 6.9 fusion.120
  464.6 10.0 multiply_convert_fusion.4
  474.6 7.2 fusion.108
  481.8 9.1 multiply_convert_fusion.6
  490.9 8.9 fusion.132
  499.8 7.0 fusion.124
  506.9 10.0 multiply_reduce_fusion.1
  528.4 8.2 multiply_convert_fusion.9
  542.7 8.6 multiply_convert_fusion.8
  560.1 10.8 multiply_convert_fusion
  577.1 9.7 multiply_convert_fusion.2
  586.8 7.2 fusion.130
  600.8 10.5 multiply_reduce_fusion
  611.3 8.1 fusion.35
  619.5 7.6 fusion.41
  634.7 39.6 %collective-permute-done.2 = bf16[1024,1024]{0,1:T(8,128)(2,1)} collective-permute-done((bf16[1024,1024]{0,1:T(8,128)(2,1)}, bf16[1024,1024]{0,1:T(8,128)(2,1)}, u32[]{:S(2)}, u32[]{:S(2)}) %collective-permute-start.2) | collective-permute-done | bytes 2097184 | tf_op jit(solution)/shard_map/ppermute | solution.py:672
  678.5 51.7 %attend_back.3 = bf16[2048,1536]{1,0:T(8,128)(2,1)} custom-call(s32[2]{0:T(128)} %pad_add_fusion.info, bf16[2048,512]{1,0:T(8,128)(2,1)} %get-tuple-element.31.q_ref, bf16[2048,512]{1,0:T(8,128)(2,1)} %get-tuple-element.32.k_ref, bf16[2048,512]{1,0:T(8,128)(2,1)} %get-tuple-element.33.v_ref, bf16[2048,512]{1,0:T(8,128)(2,1)} %get-tuple-element.26.attn_ref, ...), custom_call_target="tpu_custom_call" | custom-call | flops 25769803776 | bytes 16777216 | tf_op jit(solution)/shard_map/attend_back/pallas_call | solution.py:643
  734.4 51.3 %attend_back.2 = bf16[2048,1536]{1,0:T(8,128)(2,1)} custom-call(s32[2]{0:T(128)} %pad_add_fusion.info, bf16[2048,512]{1,0:T(8,128)(2,1)} %get-tuple-element.27.q_ref, bf16[2048,512]{1,0:T(8,128)(2,1)} %get-tuple-element.28.k_ref, bf16[2048,512]{1,0:T(8,128)(2,1)} %get-tuple-element.29.v_ref, bf16[2048,512]{1,0:T(8,128)(2,1)} %get-tuple-element.25.attn_ref, ...), custom_call_target="tpu_custom_call" | custom-call | flops 25769803776 | bytes 16777216 | tf_op jit(solution)/shard_map/attend_back/pallas_call | solution.py:643
  810.8 33.4 %collective-permute-done.3 = bf16[1024,1024]{0,1:T(8,128)(2,1)S(1)} collective-permute-done((bf16[1024,1024]{0,1:T(8,128)(2,1)S(1)}, bf16[1024,1024]{0,1:T(8,128)(2,1)S(1)}, u32[]{:S(2)}, u32[]{:S(2)}) %collective-permute-start.3) | collective-permute-done | bytes 2097184 | tf_op jit(solution)/shard_map/ppermute | solution.py:672
  909.5 7.1 fusion.220
  935.8 7.7 fusion.48
  943.6 7.1 fusion.49
  1022.6 29.1 %reduce-scatter.6.cloned.1.call-done = bf16[64,4096]{1,0:T(8,128)(2,1)} async-done(((bf16[1024,4096]{1,0:T(8,128)(2,1)}), bf16[64,4096]{1,0:T(8,128)(2,1)}) %reduce-scatter.6.cloned.1.call-update) | async-done | bytes 524304 | tf_op jit(solution)/shard_map/reduce_scatter | solution.py:680
  1054.2 183.0 %reduce-scatter.8.cloned.1.call-done = bf16[64,8448]{1,0:T(8,128)(2,1)} async-done(((bf16[1024,8448]{1,0:T(8,128)(2,1)}), bf16[64,8448]{1,0:T(8,128)(2,1)}) %reduce-scatter.8.cloned.1.call-update) | async-done | bytes 1081360 | tf_op jit(solution)/shard_map/reduce_scatter | solution.py:680
  1242.1 10.4 collective-permute-done.6
  (368 shorter events, 375.4 us)
Async XLA Ops:
  7.2 70.7 %all-gather.4.cloned.1.call-start = ((), (), s32[]{:S(2)}) async-start(), calls=%async_computation.3 | async-start | bytes 4866048 | tf_op jit(solution)/shard_map/all_gather | solution.py:702
  9.6 163.9 %all-gather.6.cloned.1.call-start = ((), (), s32[]{:S(2)}) async-start(), calls=%async_computation.4 | async-start | bytes 8650752 | tf_op jit(solution)/shard_map/all_gather | solution.py:703
  11.3 408.1 %all-gather.8.cloned.1.call-start = ((), (), s32[]{:S(2)}) async-start(), calls=%async_computation.5 | async-start | bytes 17842176 | tf_op jit(solution)/shard_map/all_gather | solution.py:706
  13.4 996.1 %reduce-scatter.4.cloned.1.call-start = ((), (), s32[]{:S(2)}) async-start(), calls=%async_computation.6 | async-start | bytes 5013504 | tf_op jit(solution)/shard_map/reduce_scatter | solution.py:853
  79.3 12.8 %copy-start.45 = (f32[1024]{0:T(1024)}, f32[1024]{0:T(1024)S(1)}, u32[]{:S(2)}) copy-start(f32[1024]{0:T(1024)S(1)} %reshape.276) | copy-start | bytes 12292
  94.6 182.7 %copy-start.23 = (bf16[1024,1024]{0,1:T(8,128)(2,1)}, bf16[1024,1024]{0,1:T(8,128)(2,1)S(1)}, u32[]{:S(2)}) copy-start(bf16[1024,1024]{0,1:T(8,128)(2,1)S(1)} %get-tuple-element.129) | copy-start | bytes 6291460
  94.6 85.1 %collective-permute-start = (bf16[1024,1024]{0,1:T(8,128)(2,1)}, bf16[1024,1024]{0,1:T(8,128)(2,1)}, u32[]{:S(2)}, u32[]{:S(2)}) collective-permute-start(bf16[1024,1024]{0,1:T(8,128)(2,1)} %get-tuple-element.128), channel_id=1, source_target_pairs={{0,1},{1,0},{2,3},{3,2},{4,5},{5,4},{6,7},{7,6},{8,9},{9,8},{10,11... | collective-permute-start | bytes 6291464 | tf_op jit(solution)/shard_map/ppermute | solution.py:672
  360.6 48.1 %collective-permute-start.1 = (bf16[1024,1024]{0,1:T(8,128)(2,1)}, bf16[1024,1024]{0,1:T(8,128)(2,1)}, u32[]{:S(2)}, u32[]{:S(2)}) collective-permute-start(bf16[1024,1024]{0,1:T(8,128)(2,1)} %add_convert_fusion.13), channel_id=1, source_target_pairs={{0,1},{1,0},{2,3},{3,2},{4,5},{5,4},{6,7},{7,6},{8,9},{9,8},{10,11... | collective-permute-start | bytes 6291464 | tf_op jit(solution)/shard_map/ppermute | solution.py:672
  366.9 96.7 %copy-start.14 = (bf16[1,1024,1024]{1,2,0:T(8,128)(2,1)}, bf16[1,1024,1024]{1,2,0:T(8,128)(2,1)S(1)}, u32[]{:S(2)}) copy-start(bf16[1,1024,1024]{1,2,0:T(8,128)(2,1)S(1)} %copy.109) | copy-start | bytes 6291460
  371.7 39.0 %copy-start.53 = (f32[1024]{0:T(1024)}, f32[1024]{0:T(1024)S(1)}, u32[]{:S(2)}) copy-start(f32[1024]{0:T(1024)S(1)} %reshape.277) | copy-start | bytes 12292
  371.8 187.3 %copy-start.43 = (f32[1024]{0:T(1024)}, f32[1024]{0:T(1024)S(1)}, u32[]{:S(2)}) copy-start(f32[1024]{0:T(1024)S(1)} %reshape.279) | copy-start | bytes 12292
  374.9 35.9 %copy-start.3 = (f32[1024,1024]{0,1:T(8,128)S(1)}, f32[1024,1024]{0,1:T(8,128)}, u32[]{:S(2)}) copy-start(f32[1024,1024]{0,1:T(8,128)} %copy-done.2) | copy-start | bytes 12582916
  374.9 35.9 %copy-start.7 = (f32[1024,1024]{0,1:T(8,128)S(1)}, f32[1024,1024]{0,1:T(8,128)}, u32[]{:S(2)}) copy-start(f32[1024,1024]{0,1:T(8,128)} %copy-done.6) | copy-start | bytes 12582916
  377.6 38.1 %copy-start.17 = (bf16[1024,1024]{0,1:T(8,128)(2,1)}, bf16[1024,1024]{0,1:T(8,128)(2,1)S(1)}, u32[]{:S(2)}) copy-start(bf16[1024,1024]{0,1:T(8,128)(2,1)S(1)} %get-tuple-element.140) | copy-start | bytes 6291460
  377.6 38.1 %copy-start.55 = (f32[1024]{0:T(1024)}, f32[1024]{0:T(1024)S(1)}, u32[]{:S(2)}) copy-start(f32[1024]{0:T(1024)S(1)} %add_rsqrt_fusion.5) | copy-start | bytes 12292
  419.5 15.5 %slice-start = ((s8[17301504]{0:T(1024)(128)(4,1)}), s8[4194304]{0:T(1024)(128)(4,1)S(1)}, s32[]{:S(2)}) async-start(s8[17301504]{0:T(1024)(128)(4,1)} %bitcast.159), calls=%async_computation.9 | async-start | bytes 8388608
  419.5 15.5 %slice-start.1 = ((s8[17301504]{0:T(1024)(128)(4,1)}), s8[4194304]{0:T(1024)(128)(4,1)S(1)}, s32[]{:S(2)}) async-start(s8[17301504]{0:T(1024)(128)(4,1)} %bitcast.159), calls=%async_computation.10 | async-start | bytes 8388608
  419.5 15.5 %slice-start.2 = ((s8[17301504]{0:T(1024)(128)(4,1)}), s8[4194304]{0:T(1024)(128)(4,1)S(1)}, s32[]{:S(2)}) async-start(s8[17301504]{0:T(1024)(128)(4,1)} %bitcast.159), calls=%async_computation.11 | async-start | bytes 8388608
  464.6 17.2 %copy-start.25 = (bf16[1024,1024]{0,1:T(8,128)(2,1)}, bf16[1024,1024]{0,1:T(8,128)(2,1)S(1)}, u32[]{:S(2)}) copy-start(bf16[1024,1024]{0,1:T(8,128)(2,1)S(1)} %fusion.21) | copy-start | bytes 6291460
  474.6 32.2 %copy-start.21 = (bf16[1024,1408]{1,0:T(8,128)(2,1)}, bf16[1024,1408]{1,0:T(8,128)(2,1)S(1)}, u32[]{:S(2)}) copy-start(bf16[1024,1408]{1,0:T(8,128)(2,1)S(1)} %get-tuple-element.94) | copy-start | bytes 8650756
  560.1 16.9 %copy-start.27 = (bf16[1024,1024]{0,1:T(8,128)(2,1)}, bf16[1024,1024]{0,1:T(8,128)(2,1)S(1)}, u32[]{:S(2)}) copy-start(bf16[1024,1024]{0,1:T(8,128)(2,1)S(1)} %fusion.18) | copy-start | bytes 6291460
  627.1 47.3 %collective-permute-start.2 = (bf16[1024,1024]{0,1:T(8,128)(2,1)}, bf16[1024,1024]{0,1:T(8,128)(2,1)}, u32[]{:S(2)}, u32[]{:S(2)}) collective-permute-start(bf16[1024,1024]{0,1:T(8,128)(2,1)} %get-tuple-element.123), channel_id=1, source_target_pairs={{0,1},{1,0},{2,3},{3,2},{4,5},{5,4},{6,7},{7,6},{8,9},{9,8},{10,11... | collective-permute-start | bytes 6291464 | tf_op jit(solution)/shard_map/ppermute | solution.py:672
  798.1 46.1 %collective-permute-start.3 = (bf16[1024,1024]{0,1:T(8,128)(2,1)S(1)}, bf16[1024,1024]{0,1:T(8,128)(2,1)S(1)}, u32[]{:S(2)}, u32[]{:S(2)}) collective-permute-start(bf16[1024,1024]{0,1:T(8,128)(2,1)S(1)} %add_convert_fusion.10), channel_id=1, source_target_pairs={{0,1},{1,0},{2,3},{3,2},{4,5},{5,4},{6,7},{7,6},{8,9},{9,8},{10,11... | collective-permute-start | bytes 6291464 | tf_op jit(solution)/shard_map/ppermute | solution.py:672
  804.0 40.2 %copy-start.4 = (f32[1024,1024]{0,1:T(8,128)S(1)}, f32[1024,1024]{0,1:T(8,128)}, u32[]{:S(2)}) copy-start(f32[1024,1024]{0,1:T(8,128)} %copy-done.2) | copy-start | bytes 12582916
  804.0 40.2 %copy-start.13 = (f32[1024,1024]{0,1:T(8,128)S(1)}, f32[1024,1024]{0,1:T(8,128)}, u32[]{:S(2)}) copy-start(f32[1024,1024]{0,1:T(8,128)} %copy-done.12) | copy-start | bytes 12582916
  804.0 40.2 %copy-start.48 = (f32[1024]{0:T(1024)S(1)}, f32[1024]{0:T(1024)}, u32[]{:S(2)}) copy-start(f32[1024]{0:T(1024)} %copy-done.47) | copy-start | bytes 12292
  871.5 180.1 %reduce-scatter.6.cloned.1.call-start = ((), (), s32[]{:S(2)}) async-start(), calls=%async_computation.7 | async-start | bytes 8912896 | tf_op jit(solution)/shard_map/reduce_scatter | solution.py:680
  908.0 329.3 %reduce-scatter.8.cloned.1.call-start = ((), (), s32[]{:S(2)}) async-start(), calls=%async_computation.8 | async-start | bytes 18382848 | tf_op jit(solution)/shard_map/reduce_scatter | solution.py:680
  1010.6 10.7 collective-permute-start.4
  1052.7 187.5 %collective-permute-start.5 = (bf16[64,2048]{1,0:T(8,128)(2,1)S(1)}, bf16[64,2048]{1,0:T(8,128)(2,1)S(1)}, u32[]{:S(2)}, u32[]{:S(2)}) collective-permute-start(bf16[64,2048]{1,0:T(8,128)(2,1)S(1)} %broadcast_select_fusion.1), channel_id=1, source_target_pairs={{0,1},{1,0},{2,3},{3,2},{4,5},{5,4},{6,7},{7,6},{8,9},{9,8},{10,11... | collective-permute-start | bytes 786440 | tf_op jit(solution)/shard_map/ppermute | solution.py:672
  1237.3 15.2 %copy-start.18 = (bf16[64,8448]{1,0:T(8,128)(2,1)S(1)}, bf16[64,8448]{1,0:T(8,128)(2,1)}, u32[]{:S(2)}) copy-start(bf16[64,8448]{1,0:T(8,128)(2,1)} %reduce-scatter.8.cloned.1.call-done) | copy-start | bytes 3244036
  1238.6 13.8 %collective-permute-start.6 = (bf16[64,4224]{1,0:T(8,128)(2,1)S(1)}, bf16[64,4224]{1,0:T(8,128)(2,1)S(1)}, u32[]{:S(2)}, u32[]{:S(2)}) collective-permute-start(bf16[64,4224]{1,0:T(8,128)(2,1)S(1)} %broadcast_select_fusion), channel_id=1, source_target_pairs={{0,1},{1,0},{2,3},{3,2},{4,5},{5,4},{6,7},{7,6},{8,9},{9,8},{10,11... | collective-permute-start | bytes 1622024 | tf_op jit(solution)/shard_map/ppermute | solution.py:672
  (82 other events, 441.8 us)
Sparse Core Ops, SparseCore 0:
  11.5 66.3 all-gather.3
  81.2 92.2 all-gather.5
  176.4 115.2 all-gather.7
  871.6 73.4 reduce-scatter.3
  949.0 102.5 reduce-scatter.5
  1055.6 181.5 reduce-scatter.7
